TPU v7x, 256 devices: a whole 4x4x8 slice. The times are simulated.
256 devices in a mesh: pop: 64 (over x, z, core), mp: 4 (over y).
Axes of the slice: x: 4, y: 4, z: 8, core: 2. Of those that a mesh axis runs over, the one named last changes fastest.
Arguments:
- tokens: bfloat16 [256, 3584], replicated, may hold values from -60 to 60
- target: bfloat16 [256, 3584], P(None, 'mp'), may hold values from -6 to 6
- w_query: bfloat16 [3584, 3584], P('pop', 'mp'), may hold values from -0.09375 to 0.09375
- w_key: bfloat16 [3584, 512], P(None, 'mp'), may hold values from -0.09375 to 0.09375
- w_value: bfloat16 [3584, 512], P(None, 'mp'), may hold values from -0.09375 to 0.09375
- w_out: bfloat16 [3584, 3584], P('mp', 'pop'), may hold values from -0.09375 to 0.09375
- query_left_factors: bfloat16 [64, 3584, 4], P('pop'), may hold values from -0.09375 to 0.09375
- query_right_factors: bfloat16 [64, 4, 3584], P('pop', None, 'mp'), may hold values from -6 to 6
- o_left: bfloat16 [64, 3584, 4], P('pop', 'mp'), may hold values from -0.09375 to 0.09375
- o_right: bfloat16 [64, 4, 3584], P('pop'), may hold values from -6 to 6
- member_ids: int32 [64], P('pop'), may hold values from 0 to 63, each once
Outputs:
- grad_query: float32 [3584, 3584], P('pop', 'mp')
- grad_out: float32 [3584, 3584], P('mp', 'pop')
- fitness: float32 [64], P('pop')
Inputs may be any that keep to these rules, and one draw needn't show every extreme that they name: `member_ids`: every number from 0 to 63 appears once.
All inputs are finite; a program needn't handle non-finite values.
Results may differ from a plain program's by a relative error of at most 0.005.
Values may be sent and summed in bfloat16 or wider, within the bound.
No kernel may reach another device: no remote copies, remote signals or barrier semaphores. Data moves between devices by JAX's collectives and lax.ppermute only.
A program may use at most 64 MiB of HBM per device.

v0:
```python
import math
import jax
import jax.numpy as jnp
from jax import lax
from jax.sharding import Mesh
from jax.sharding import PartitionSpec as P

D = 3584
HEADS = 28
KV_HEADS = 4
HEAD_DIM = 128
RANK = 4
POP = ("pop_0", "pop_1", "pop_2")
noise_scale = 0.5
rope_base = 1000000.0
spread_floor = 0.001


def in_order(parts, dim):
    parts = jnp.moveaxis(parts, 0, dim)
    shape = parts.shape
    return parts.reshape(*shape[:dim], shape[dim] * shape[dim + 1], *shape[dim + 2 :])


def all_blocks(shard, axes, turns):
    parts = shard[None]
    for k in turns:
        parts = lax.all_gather(parts, axes[k], axis=0, tiled=True)
    held = [lax.axis_size(axes[k]) for k in reversed(turns)]
    parts = parts.reshape(*held, *shard.shape)
    turned = sorted(range(len(turns)), key=lambda place: turns[len(turns) - 1 - place])
    return parts.transpose(*turned, *range(len(turns), parts.ndim)).reshape(-1, *shard.shape)


def whole_of(shard, axes, turns, dim):
    return in_order(all_blocks(shard, axes, turns), dim)


def cut_along(shard, dim, devices):
    before, after = (shard.shape[:dim], shard.shape[dim + 1 :])
    return jnp.moveaxis(shard.reshape(*before, devices, -1, *after), dim, 0)


def summed_on_arrival(shard, axis, dim):
    devices = lax.axis_size(axis)
    parts = lax.all_to_all(cut_along(shard, dim, devices), axis, 0, 0, tiled=True)
    return jnp.sum(parts.astype(jnp.float32), axis=0)


def copy_for_each(shard, axis):
    copies = jnp.broadcast_to(shard, (lax.axis_size(axis), *shard.shape))
    return lax.all_to_all(copies, axis, split_axis=0, concat_axis=0, tiled=True)


def of_everyone(shard, axis):
    return copy_for_each(shard, axis).sum(axis=0)


def gathered_copies(shard, axis, dim):
    return in_order(copy_for_each(shard, axis), dim)


def side_by_side(arrays, axis, dim, along):
    columns = [a.reshape(*a.shape[:along], -1) for a in arrays]
    both = jnp.concatenate(columns, axis=along)
    result, at, done = (lax.all_gather(both, axis, axis=dim, tiled=True), 0, [])
    for a, column in zip(arrays, columns):
        share = result[..., at : at + column.shape[along]]
        done.append(share.reshape(*share.shape[:along], *a.shape[along:]))
        at += column.shape[along]
    return tuple(done)


def tables(count, head_size):
    position = jnp.arange(count, dtype=jnp.float32)
    index = jnp.arange(head_size // 2, dtype=jnp.float32)
    freq = jnp.exp(-math.log(rope_base) * 2.0 * index / head_size)
    angle = position[:, None] * freq[None, :]
    return (jnp.cos(angle)[:, None, :], jnp.sin(angle)[:, None, :])


def rotate(field, cosine_table, sine):
    half = field.shape[-1] // 2
    first = field[..., :half]
    second = field[..., half:]
    return jnp.concatenate(
        [first * cosine_table - second * sine, second * cosine_table + first * sine], axis=-1
    )


def per_device(
    tokens,
    target,
    w_query,
    w_key,
    w_value,
    w_out,
    query_left_factors,
    query_right_factors,
    o_left,
    o_right,
    member_ids,
):
    tok = tokens.shape[0]
    local_feats = w_query.shape[1]
    local_kv = w_key.shape[1] // HEAD_DIM
    group = HEADS // KV_HEADS
    local_heads = local_kv * group
    slots = query_left_factors.shape[0]
    scale = HEAD_DIM ** (-0.5)
    cosine_table, sine = tables(tok, HEAD_DIM)
    base = jnp.dot(tokens, whole_of(w_query, POP, (0, 1, 2), 0), preferred_element_type=jnp.float32)
    keys = rotate(
        jnp.dot(tokens, w_key, preferred_element_type=jnp.float32).reshape(tok, local_kv, HEAD_DIM),
        cosine_table,
        sine,
    ).astype(jnp.bfloat16)
    values = (
        jnp.dot(tokens, w_value, preferred_element_type=jnp.float32)
        .astype(jnp.bfloat16)
        .reshape(tok, local_kv, HEAD_DIM)
    )
    signs = (1 - 2 * (member_ids % 2)).astype(jnp.float32)
    factor = noise_scale * signs[:, None, None]
    lowrank_product = jnp.einsum(
        "td,mdr->mtr", tokens, query_left_factors, preferred_element_type=jnp.float32
    ).astype(jnp.bfloat16)
    query = base[None] + factor * jnp.einsum(
        "olj,ojv->olv", lowrank_product, query_right_factors, preferred_element_type=jnp.float32
    )
    query = rotate(
        query.reshape(slots, tok, local_heads, HEAD_DIM), cosine_table[None], sine[None]
    ).astype(jnp.bfloat16)
    query = query.reshape(slots, tok, local_kv, group, HEAD_DIM)
    scores = jnp.einsum("mtkgd,skd->mkgts", query, keys, preferred_element_type=jnp.float32) * scale
    causal = jnp.arange(tok)[:, None] >= jnp.arange(tok)[None, :]
    scores = jnp.where(causal, scores, -1e30)
    probs = jax.nn.softmax(scores, axis=-1).astype(jnp.bfloat16)
    mixed = (
        jnp.einsum("mkgts,skd->mtkgd", probs, values, preferred_element_type=jnp.float32)
        .astype(jnp.bfloat16)
        .reshape(slots, tok, local_feats)
    )
    low_out = jnp.einsum("mtf,mfr->mtr", mixed, o_left, preferred_element_type=jnp.float32)
    right_full = o_right.astype(jnp.float32)
    part = jnp.einsum(
        "mtf,fe->mte",
        mixed,
        lax.all_gather(w_out, POP, axis=1, tiled=True),
        preferred_element_type=jnp.float32,
    )
    term = part + factor * jnp.einsum(
        "mtr,mre->mte", low_out, right_full, precision=lax.Precision.HIGHEST
    )
    output = summed_on_arrival(term.astype(jnp.bfloat16), "mp", 2)
    diff = output - target.astype(jnp.float32)[None]
    errors = of_everyone(jnp.sum(diff * diff, axis=(1, 2)), "mp")
    fitness = -(errors / (tok * D))
    count = slots * lax.axis_size(POP)
    everyone = gathered_copies(fitness, POP, 0)
    mean = jnp.sum(everyone) / count
    spread = jnp.sum((everyone - mean) * (everyone - mean)) / count
    weight = signs * (fitness - mean) / jnp.sqrt(spread + spread_floor)
    every_weight = gathered_copies(weight, POP, 0)
    right_factors_gathered, left_all = side_by_side((query_right_factors, o_left), POP, 0, 1)
    rows_q = lax.all_to_all(query_left_factors, POP, split_axis=1, concat_axis=0, tiled=True)
    cols_o = lax.all_to_all(o_right, POP, split_axis=2, concat_axis=0, tiled=True)
    whole_population = rows_q.shape[0]
    left_q = jnp.transpose(
        rows_q.astype(jnp.float32) * every_weight[:, None, None], (1, 0, 2)
    ).reshape(rows_q.shape[1], whole_population * RANK)
    right_q = right_factors_gathered.astype(jnp.float32).reshape(
        whole_population * RANK, local_feats
    )
    grad_query = jnp.dot(left_q, right_q, precision=lax.Precision.HIGHEST) / noise_scale
    output_left_factor = jnp.transpose(
        left_all.astype(jnp.float32) * every_weight[:, None, None], (1, 0, 2)
    ).reshape(local_feats, whole_population * RANK)
    right_o = cols_o.astype(jnp.float32).reshape(whole_population * RANK, cols_o.shape[2])
    grad_out = jnp.dot(output_left_factor, right_o, precision=lax.Precision.HIGHEST) / noise_scale
    return (grad_query, grad_out, fitness)


def solution(mesh):
    torus = Mesh(mesh.devices.reshape(4, 8, 2, mesh.shape["mp"]), ("pop_0", "pop_1", "pop_2", "mp"))
    placed = (
        P(),
        P(None, "mp"),
        P(POP, "mp"),
        P(None, "mp"),
        P(None, "mp"),
        P("mp", POP),
        P(POP, None, None),
        P(POP, None, "mp"),
        P(POP, "mp", None),
        P(POP, None, None),
        P(POP),
    )
    return jax.shard_map(
        per_device,
        mesh=torus,
        in_specs=placed,
        out_specs=(P(POP, "mp"), P("mp", POP), P(POP)),
        check_vma=False,
    )
```

profile of v0, /device:TPU:1, one launch (start us, length us, event | category | flops | bytes accessed | tf_op | source)
XLA Modules:
  0.0 428.7 jit_solution(7784847421207332163)
XLA Ops:
  7.2 13.0 %all-gather = bf16[224,896]{1,0:T(8,128)(2,1)} all-gather(bf16[56,896]{1,0:T(8,128)(2,1)} %param.13), channel_id=2, replica_groups=mesh['pop_0'=4,'pop_1'=8,'pop_2'=2,'mp'=4] {'pop_0'}, dimensions={0}, use_global_device_ids=true | all-gather | bytes 501760 | tf_op jit(solution)/shard_map/all_gather | solution.py:28
  20.3 49.6 %all-gather.6.cloned.1.call-done = bf16[32,56,896]{2,1,0:T(8,128)(2,1)} async-done(((bf16[4,56,896]{2,1,0:T(8,128)(2,1)}), bf16[32,56,896]{2,1,0:T(8,128)(2,1)}) %all-gather.6.cloned.1.call-update) | async-done | bytes 3211280 | tf_op jit(solution)/shard_map/all_gather | solution.py:28
  73.6 19.9 %all-gather.8.cloned.1.call-done = bf16[64,56,896]{2,1,0:T(8,128)(2,1)} async-done(((bf16[32,56,896]{2,1,0:T(8,128)(2,1)}), bf16[64,56,896]{2,1,0:T(8,128)(2,1)}) %all-gather.8.cloned.1.call-update) | async-done | bytes 6422544 | tf_op jit(solution)/shard_map/all_gather | solution.py:28
  93.5 3.3 copy.114
  96.9 2.1 fusion.29
  99.1 2.1 fusion.3
  101.1 1.5 copy.115
  110.0 2.6 convolution_convert_fusion
  112.8 65.1 %all-gather.10.cloned.1.call-done = bf16[896,3584]{0,1:T(8,128)(2,1)} async-done(((bf16[896,56]{0,1:T(8,128)(2,1)}), bf16[896,3584]{0,1:T(8,128)(2,1)}) %all-gather.10.cloned.1.call-update) | async-done | bytes 6422544 | tf_op jit(solution)/shard_map/all_gather | solution.py:149
  177.9 4.9 %fusion.30 = f32[256,3584]{1,0:T(8,128)S(1)} fusion(bf16[256,896]{0,1:T(8,128)(2,1)S(1)} %bitcast.106, bf16[896,3584]{0,1:T(8,128)(2,1)} %all-gather.10.cloned.1.call-done), kind=kOutput, calls=%fused_computation.58 | convolution fusion | flops 1644167168 | bytes 10551296 | tf_op jit(solution)/shard_map/mtf,fe->mte/dot_general | solution.py:146
  182.8 3.1 fusion.1
  185.9 3.3 reshape.288
  189.2 1.5 copy.145
  190.7 4.0 all-to-all-start.1
  195.3 22.5 %all-to-all-done.1 = bf16[4,1,256,896]{3,2,1,0:T(8,128)(2,1)S(1)} async-done(((bf16[4,1,256,896]{3,2,1,0:T(8,128)(2,1)}), bf16[4,1,256,896]{3,2,1,0:T(8,128)(2,1)S(1)}, u32[]{:S(2)}, u32[]{:S(2)}) %all-to-all-start.1) | async-done | bytes 1835040 | tf_op jit(solution)/shard_map/all_to_all | solution.py:46
  219.6 6.5 %all_to_all.47 = f32[4,1,1]{2,1,0:T(1,128)S(1)} all-to-all(f32[4,1,1]{2,1,0:T(1,128)S(1)} %broadcast_in_dim.34), channel_id=1, replica_groups=mesh['pop_0'=4,'pop_1'=8,'pop_2'=2,'mp'=4] {'mp'}, dimensions={0} | all-to-all | bytes 32 | tf_op jit(solution)/shard_map/all_to_all | solution.py:52
  227.9 7.9 %all-to-all-start.3 = ((f32[64,1,1]{2,1,0:T(1,128)}), f32[64,1,1]{2,1,0:T(1,128)S(1)}, u32[]{:S(2)}, u32[]{:S(2)}) async-start(f32[64,1,1]{2,1,0:T(1,128)} %broadcast_in_dim.35), calls=%async_computation.3 | async-start | bytes 65536 | tf_op jit(solution)/shard_map/all_to_all | solution.py:52
  235.9 51.8 %all-gather.1 = bf16[64,1,7168]{2,1,0:T(2,128)(2,1)S(1)} all-gather(bf16[1,1,7168]{2,1,0:T(2,128)(2,1)S(1)} %maximum_bitcast_fusion.2), channel_id=1, replica_groups=mesh['pop_0'=4,'pop_1'=8,'pop_2'=2,'mp'=4] {'pop_0','pop_1','pop_2'}, dimensions={0}, use_global_device_ids=true | all-gather | bytes 931840 | tf_op jit(solution)/shard_map/all_gather | solution.py:66
  287.7 3.2 copy.129
  292.2 7.3 %all-to-all-start.5 = ((bf16[1,4,3584]{1,0,2:T(2,128)(2,1)}), bf16[1,4,3584]{1,0,2:T(2,128)(2,1)S(1)}, u32[]{:S(2)}, u32[]{:S(2)}) async-start(bf16[1,4,3584]{1,0,2:T(2,128)(2,1)} %copy.129), calls=%async_computation.5 | async-start | bytes 3670016 | tf_op jit(solution)/shard_map/all_to_all | solution.py:167
  299.4 2.0 slice_convert_fusion
  301.5 3.2 copy.112
  306.1 38.7 %all-to-all-done.5 = bf16[1,4,3584]{1,0,2:T(2,128)(2,1)S(1)} async-done(((bf16[1,4,3584]{1,0,2:T(2,128)(2,1)}), bf16[1,4,3584]{1,0,2:T(2,128)(2,1)S(1)}, u32[]{:S(2)}, u32[]{:S(2)}) %all-to-all-start.5) | async-done | bytes 28704 | tf_op jit(solution)/shard_map/all_to_all | solution.py:167
  344.8 6.2 %all-to-all-start = ((bf16[1,3584,4]{2,0,1:T(2,128)(2,1)}), bf16[1,3584,4]{2,0,1:T(2,128)(2,1)}, u32[]{:S(2)}, u32[]{:S(2)}) async-start(bf16[1,3584,4]{2,0,1:T(2,128)(2,1)} %copy.112), calls=%async_computation | async-start | bytes 3670016 | tf_op jit(solution)/shard_map/all_to_all | solution.py:166
  352.3 44.0 %all-to-all-done = bf16[1,3584,4]{2,0,1:T(2,128)(2,1)} async-done(((bf16[1,3584,4]{2,0,1:T(2,128)(2,1)}), bf16[1,3584,4]{2,0,1:T(2,128)(2,1)}, u32[]{:S(2)}, u32[]{:S(2)}) %all-to-all-start) | async-done | bytes 28704 | tf_op jit(solution)/shard_map/all_to_all | solution.py:166
  396.9 6.0 %all-to-all-start.4 = ((f32[64,1,1]{2,1,0:T(1,128)}), f32[64,1,1]{2,1,0:T(1,128)S(1)}, u32[]{:S(2)}, u32[]{:S(2)}) async-start(f32[64,1,1]{2,1,0:T(1,128)} %broadcast_in_dim.36), calls=%async_computation.4 | async-start | bytes 65536 | tf_op jit(solution)/shard_map/all_to_all | solution.py:52
  403.0 1.8 copy.127
  406.0 1.8 copy.130
  408.1 3.7 copy.113
  412.8 1.6 multiply_bitcast_fusion
  414.4 2.8 copy.128
  417.2 1.5 reshape.293
  (71 shorter events, 22.1 us)
Async XLA Ops:
  7.2 64.2 %copy-start = (bf16[256,3584]{1,0:T(8,128)(2,1)S(1)}, bf16[256,3584]{1,0:T(8,128)(2,1)}, u32[]{:S(2)}) copy-start(bf16[256,3584]{1,0:T(8,128)(2,1)} %param.11) | copy-start | bytes 5505028
  7.2 62.7 %all-gather.6.cloned.1.call-start = ((), (), s32[]{:S(2)}) async-start(), calls=%async_computation.6 | async-start | bytes 3612672 | tf_op jit(solution)/shard_map/all_gather | solution.py:28
  20.2 51.2 %copy-start.4 = (bf16[3584,128]{1,0:T(8,128)(2,1)S(1)}, bf16[3584,128]{1,0:T(8,128)(2,1)}, u32[]{:S(2)}) copy-start(bf16[3584,128]{1,0:T(8,128)(2,1)} %param.14) | copy-start | bytes 2752516
  20.3 73.3 %all-gather.8.cloned.1.call-start = ((), (), s32[]{:S(2)}) async-start(), calls=%async_computation.7 | async-start | bytes 9633792 | tf_op jit(solution)/shard_map/all_gather | solution.py:28
  69.9 107.9 %all-gather.10.cloned.1.call-start = ((), (), s32[]{:S(2)}) async-start(), calls=%async_computation.8 | async-start | bytes 6522880 | tf_op jit(solution)/shard_map/all_gather | solution.py:149
  96.9 2.2 copy-start.9
  96.9 2.2 copy-start.11
  106.1 1.4 copy-start.6
  106.1 1.4 copy-start.7
  108.1 1.3 copy-start.2
  108.2 1.9 copy-start.13
  110.0 2.6 copy-start.12
  112.8 70.0 %copy-start.8 = (bf16[1,4,3584]{2,1,0:T(4,128)(2,1)S(1)}, bf16[1,4,3584]{2,1,0:T(4,128)(2,1)}, u32[]{:S(2)}) copy-start(bf16[1,4,3584]{2,1,0:T(4,128)(2,1)} %param.20) | copy-start | bytes 86020
  190.7 27.1 %all-to-all-start.1 = ((bf16[4,1,256,896]{3,2,1,0:T(8,128)(2,1)}), bf16[4,1,256,896]{3,2,1,0:T(8,128)(2,1)S(1)}, u32[]{:S(2)}, u32[]{:S(2)}) async-start(bf16[4,1,256,896]{3,2,1,0:T(8,128)(2,1)} %bitcast.98), calls=%async_computation.1 | async-start | bytes 3670016 | tf_op jit(solution)/shard_map/all_to_all | solution.py:46
  194.7 23.3 %copy-start.5 = (bf16[256,896]{1,0:T(8,128)(2,1)S(1)}, bf16[256,896]{1,0:T(8,128)(2,1)}, u32[]{:S(2)}) copy-start(bf16[256,896]{1,0:T(8,128)(2,1)} %param.12) | copy-start | bytes 1376260
  227.9 64.2 %all-to-all-start.3 = ((f32[64,1,1]{2,1,0:T(1,128)}), f32[64,1,1]{2,1,0:T(1,128)S(1)}, u32[]{:S(2)}, u32[]{:S(2)}) async-start(f32[64,1,1]{2,1,0:T(1,128)} %broadcast_in_dim.35), calls=%async_computation.3 | async-start | bytes 65536 | tf_op jit(solution)/shard_map/all_to_all | solution.py:52
  292.2 52.6 %all-to-all-start.5 = ((bf16[1,4,3584]{1,0,2:T(2,128)(2,1)}), bf16[1,4,3584]{1,0,2:T(2,128)(2,1)S(1)}, u32[]{:S(2)}, u32[]{:S(2)}) async-start(bf16[1,4,3584]{1,0,2:T(2,128)(2,1)} %copy.129), calls=%async_computation.5 | async-start | bytes 3670016 | tf_op jit(solution)/shard_map/all_to_all | solution.py:167
  299.4 2.1 copy-start.10
  344.8 51.5 %all-to-all-start = ((bf16[1,3584,4]{2,0,1:T(2,128)(2,1)}), bf16[1,3584,4]{2,0,1:T(2,128)(2,1)}, u32[]{:S(2)}, u32[]{:S(2)}) async-start(bf16[1,3584,4]{2,0,1:T(2,128)(2,1)} %copy.112), calls=%async_computation | async-start | bytes 3670016 | tf_op jit(solution)/shard_map/all_to_all | solution.py:166
  396.9 15.3 %all-to-all-start.4 = ((f32[64,1,1]{2,1,0:T(1,128)}), f32[64,1,1]{2,1,0:T(1,128)S(1)}, u32[]{:S(2)}, u32[]{:S(2)}) async-start(f32[64,1,1]{2,1,0:T(1,128)} %broadcast_in_dim.36), calls=%async_computation.4 | async-start | bytes 65536 | tf_op jit(solution)/shard_map/all_to_all | solution.py:52
  407.9 4.9 %copy-start.3 = (f32[64,3584]{0,1:T(8,128)S(1)}, f32[64,3584]{0,1:T(8,128)}, u32[]{:S(2)}) copy-start(f32[64,3584]{0,1:T(8,128)} %copy.127) | copy-start | bytes 2752516
  414.3 6.7 %copy-start.1 = (bf16[256,3584]{1,0:T(8,128)(2,1)S(1)}, bf16[256,3584]{1,0:T(8,128)(2,1)}, u32[]{:S(2)}) copy-start(bf16[256,3584]{1,0:T(8,128)(2,1)} %param.11) | copy-start | bytes 5505028
Sparse Core Ops, SparseCore 0:
  20.4 49.4 all-gather.5
  71.7 21.7 all-gather.7
  96.2 81.5 all-gather.9
where the time goes:
time: 430 us; the launch traced here: 429 us
  waiting for transfers between devices  241 us (56%)
  blocking collectives  71.3 us (17%)
  local copies, waits for them, and re-layouts  38.2 us (9%)
  starting transfers between devices  31.5 us (7%)
  matrix products  18.6 us (4%)
  between operations  17.9 us (4%)
  other arithmetic  10.5 us (2%)
    all_gather x2, waiting for transfers between devices, all_blocks(): parts = lax.all_gather(parts, axes[k], axis=0, tiled=True)  69.5 us
    all_gather x1, waiting for transfers between devices, per_device(): lax.all_gather(w_out, POP, axis=1, tiled=True)  65.1 us
    all_gather x1, blocking collectives, side_by_side(): result, at, done = (lax.all_gather(both, axis, axis=dim, tiled=True), 0, [])  51.8 us
    all_to_all x1, waiting for transfers between devices, per_device(): lax.all_to_all(query_left_factors, POP, split_axis=1, concat_axis=0, tile...  44 us
    all_to_all x1, waiting for transfers between devices, per_device(): lax.all_to_all(o_right, POP, split_axis=2, concat_axis=0, tiled=True)  38.7 us
    all_to_all x1, waiting for transfers between devices, summed_on_arrival(): lax.all_to_all(cut_along(shard, dim, devices), axis, 0, 0, tiled=True)  22.5 us
    all_to_all x2, starting transfers between devices, copy_for_each(): return lax.all_to_all(copies, axis, split_axis=0, concat_axis=0, tiled=True)  14 us
    all_gather x1, blocking collectives, all_blocks(): parts = lax.all_gather(parts, axes[k], axis=0, tiled=True)  13 us
  transfers between devices with their start and end apart: 8, of which 7 were waited for; matrix products, arithmetic and copies ran while one was open for 9% of the time, Pallas kernels for 0%

commit v1 on v0

--- a/solution.py
+++ b/solution.py
@@ -14,6 +14,11 @@
 noise_scale = 0.5
 rope_base = 1000000.0
 spread_floor = 0.001
+
+
+def gather_over(array, name, dim):
+    stack = jnp.stack([array] * lax.axis_size(name))
+    return jnp.concatenate(lax.all_to_all(stack, name, 0, 0), axis=dim)
 
 
 def in_order(parts, dim):
@@ -144,10 +149,7 @@
     low_out = jnp.einsum("mtf,mfr->mtr", mixed, o_left, preferred_element_type=jnp.float32)
     right_full = o_right.astype(jnp.float32)
     part = jnp.einsum(
-        "mtf,fe->mte",
-        mixed,
-        lax.all_gather(w_out, POP, axis=1, tiled=True),
-        preferred_element_type=jnp.float32,
+        "mtf,fe->mte", mixed, gather_over(w_out, POP, 1), preferred_element_type=jnp.float32
     )
     term = part + factor * jnp.einsum(
         "mtr,mre->mte", low_out, right_full, precision=lax.Precision.HIGHEST

time: 430 us -> 462 us (1.074)
  waiting for transfers between devices: 241 us -> 255 us
  starting transfers between devices: 31.5 us -> 44.8 us
    all_gather x1 -> x0, waiting for transfers between devices: 65.1 us -> none  [per_device(): lax.all_gather(w_out, POP, axis=1, tiled=True)]
    all_gather x2, waiting for transfers between devices: 69.5 us -> 128 us  [all_blocks(): parts = lax.all_gather(parts, axes[k], axis=0, tiled=True)]
    all_to_all x0 -> x1, waiting for transfers between devices: none -> 21.6 us  [gather_over(): return jnp.concatenate(lax.all_to_all(stack, name, 0, 0), axis=dim)]
    all_to_all x0 -> x1, starting transfers between devices: none -> 13.5 us  [gather_over(): return jnp.concatenate(lax.all_to_all(stack, name, 0, 0), axis=dim)]
  transfers between devices with their start and end apart: 8 -> 8, of which waited for: 7 -> 7; matrix products, arithmetic and copies ran while one was open for 9% -> 10% of each run, Pallas kernels for 0% -> 0%
where the time goes in v1:
time: 462 us; the launch traced here: 461 us
  waiting for transfers between devices  255 us (55%)
  blocking collectives  71.3 us (15%)
  starting transfers between devices  44.8 us (10%)
  local copies, waits for them, and re-layouts  42.4 us (9%)
  matrix products  18.6 us (4%)
  between operations  18.3 us (4%)
  other arithmetic  10.5 us (2%)
    all_gather x2, waiting for transfers between devices, all_blocks(): parts = lax.all_gather(parts, axes[k], axis=0, tiled=True)  128 us
    all_gather x1, blocking collectives, side_by_side(): result, at, done = (lax.all_gather(both, axis, axis=dim, tiled=True), 0, [])  51.8 us
    all_to_all x1, waiting for transfers between devices, per_device(): lax.all_to_all(query_left_factors, POP, split_axis=1, concat_axis=0, tile...  44 us
    all_to_all x1, waiting for transfers between devices, per_device(): lax.all_to_all(o_right, POP, split_axis=2, concat_axis=0, tiled=True)  38.8 us
    all_to_all x1, waiting for transfers between devices, summed_on_arrival(): lax.all_to_all(cut_along(shard, dim, devices), axis, 0, 0, tiled=True)  22.4 us
    all_to_all x1, waiting for transfers between devices, gather_over(): return jnp.concatenate(lax.all_to_all(stack, name, 0, 0), axis=dim)  21.6 us
    all_to_all x2, starting transfers between devices, copy_for_each(): return lax.all_to_all(copies, axis, split_axis=0, concat_axis=0, tiled=True)  13.8 us
    all_to_all x1, starting transfers between devices, gather_over(): return jnp.concatenate(lax.all_to_all(stack, name, 0, 0), axis=dim)  13.5 us
  transfers between devices with their start and end apart: 8, of which 7 were waited for; matrix products, arithmetic and copies ran while one was open for 10% of the time, Pallas kernels for 0%

profile of v1, /device:TPU:1, one launch (start us, length us, event | category | flops | bytes accessed | tf_op | source)
XLA Modules:
  0.0 460.7 jit_solution(10587158637562555518)
XLA Ops:
  7.2 13.0 %all-gather = bf16[224,896]{1,0:T(8,128)(2,1)} all-gather(bf16[56,896]{1,0:T(8,128)(2,1)} %param.13), channel_id=2, replica_groups=mesh['pop_0'=4,'pop_1'=8,'pop_2'=2,'mp'=4] {'pop_0'}, dimensions={0}, use_global_device_ids=true | all-gather | bytes 501760 | tf_op jit(solution)/shard_map/all_gather | solution.py:33
  20.3 4.0 stack.2
  24.3 13.5 %all-to-all-start.1 = ((bf16[64,896,56]{1,2,0:T(8,128)(2,1)}), bf16[64,896,56]{1,2,0:T(8,128)(2,1)}, u32[]{:S(2)}, u32[]{:S(2)}) async-start(bf16[64,896,56]{1,2,0:T(8,128)(2,1)} %stack.2), calls=%async_computation.1 | async-start | bytes 12845056 | tf_op jit(solution)/shard_map/all_to_all | solution.py:21
  37.8 104.5 %all-gather.5.cloned.1.call-done = bf16[32,56,896]{2,1,0:T(8,128)(2,1)} async-done(((bf16[4,56,896]{2,1,0:T(8,128)(2,1)}), bf16[32,56,896]{2,1,0:T(8,128)(2,1)}) %all-gather.5.cloned.1.call-update) | async-done | bytes 3211280 | tf_op jit(solution)/shard_map/all_gather | solution.py:33
  145.3 23.5 %all-gather.7.cloned.1.call-done = bf16[64,56,896]{2,1,0:T(8,128)(2,1)} async-done(((bf16[32,56,896]{2,1,0:T(8,128)(2,1)}), bf16[64,56,896]{2,1,0:T(8,128)(2,1)}) %all-gather.7.cloned.1.call-update) | async-done | bytes 6422544 | tf_op jit(solution)/shard_map/all_gather | solution.py:33
  168.8 3.3 copy.115
  172.2 2.1 fusion.29
  174.4 2.1 fusion.3
  185.5 2.6 convolution_convert_fusion
  188.2 21.6 %all-to-all-done.1 = bf16[64,896,56]{1,2,0:T(8,128)(2,1)} async-done(((bf16[64,896,56]{1,2,0:T(8,128)(2,1)}), bf16[64,896,56]{1,2,0:T(8,128)(2,1)}, u32[]{:S(2)}, u32[]{:S(2)}) %all-to-all-start.1) | async-done | bytes 6422560 | tf_op jit(solution)/shard_map/all_to_all | solution.py:21
  209.8 4.9 %fusion.30 = f32[256,3584]{1,0:T(8,128)S(1)} fusion(bf16[256,896]{0,1:T(8,128)(2,1)S(1)} %bitcast.109, bf16[896,3584]{0,1:T(8,128)(2,1)} %bitcast.25), kind=kOutput, calls=%fused_computation.58 | convolution fusion | flops 1644167168 | bytes 10551296 | tf_op jit(solution)/shard_map/mtf,fe->mte/dot_general | solution.py:151
  214.7 3.1 fusion.1
  217.8 3.3 reshape.298
  221.2 1.5 copy.146
  222.7 4.0 all-to-all-start.2
  227.2 22.4 %all-to-all-done.2 = bf16[4,1,256,896]{3,2,1,0:T(8,128)(2,1)S(1)} async-done(((bf16[4,1,256,896]{3,2,1,0:T(8,128)(2,1)}), bf16[4,1,256,896]{3,2,1,0:T(8,128)(2,1)S(1)}, u32[]{:S(2)}, u32[]{:S(2)}) %all-to-all-start.2) | async-done | bytes 1835040 | tf_op jit(solution)/shard_map/all_to_all | solution.py:51
  251.4 6.5 %all_to_all.52 = f32[4,1,1]{2,1,0:T(1,128)S(1)} all-to-all(f32[4,1,1]{2,1,0:T(1,128)S(1)} %broadcast_in_dim.34), channel_id=1, replica_groups=mesh['pop_0'=4,'pop_1'=8,'pop_2'=2,'mp'=4] {'mp'}, dimensions={0} | all-to-all | bytes 32 | tf_op jit(solution)/shard_map/all_to_all | solution.py:57
  259.8 7.8 %all-to-all-start.4 = ((f32[64,1,1]{2,1,0:T(1,128)}), f32[64,1,1]{2,1,0:T(1,128)S(1)}, u32[]{:S(2)}, u32[]{:S(2)}) async-start(f32[64,1,1]{2,1,0:T(1,128)} %broadcast_in_dim.35), calls=%async_computation.4 | async-start | bytes 65536 | tf_op jit(solution)/shard_map/all_to_all | solution.py:57
  267.5 51.8 %all-gather.1 = bf16[64,1,7168]{2,1,0:T(2,128)(2,1)S(1)} all-gather(bf16[1,1,7168]{2,1,0:T(2,128)(2,1)S(1)} %maximum_bitcast_fusion.2), channel_id=1, replica_groups=mesh['pop_0'=4,'pop_1'=8,'pop_2'=2,'mp'=4] {'pop_0','pop_1','pop_2'}, dimensions={0}, use_global_device_ids=true | all-gather | bytes 931840 | tf_op jit(solution)/shard_map/all_gather | solution.py:71
  319.4 3.2 copy.130
  323.8 7.3 %all-to-all-start.6 = ((bf16[1,4,3584]{1,0,2:T(2,128)(2,1)}), bf16[1,4,3584]{1,0,2:T(2,128)(2,1)S(1)}, u32[]{:S(2)}, u32[]{:S(2)}) async-start(bf16[1,4,3584]{1,0,2:T(2,128)(2,1)} %copy.130), calls=%async_computation.6 | async-start | bytes 3670016 | tf_op jit(solution)/shard_map/all_to_all | solution.py:169
  331.1 2.0 slice_convert_fusion
  333.1 3.2 copy.113
  337.7 38.8 %all-to-all-done.6 = bf16[1,4,3584]{1,0,2:T(2,128)(2,1)S(1)} async-done(((bf16[1,4,3584]{1,0,2:T(2,128)(2,1)}), bf16[1,4,3584]{1,0,2:T(2,128)(2,1)S(1)}, u32[]{:S(2)}, u32[]{:S(2)}) %all-to-all-start.6) | async-done | bytes 28704 | tf_op jit(solution)/shard_map/all_to_all | solution.py:169
  376.5 6.2 %all-to-all-start = ((bf16[1,3584,4]{2,0,1:T(2,128)(2,1)}), bf16[1,3584,4]{2,0,1:T(2,128)(2,1)}, u32[]{:S(2)}, u32[]{:S(2)}) async-start(bf16[1,3584,4]{2,0,1:T(2,128)(2,1)} %copy.113), calls=%async_computation | async-start | bytes 3670016 | tf_op jit(solution)/shard_map/all_to_all | solution.py:168
  384.0 44.0 %all-to-all-done = bf16[1,3584,4]{2,0,1:T(2,128)(2,1)} async-done(((bf16[1,3584,4]{2,0,1:T(2,128)(2,1)}), bf16[1,3584,4]{2,0,1:T(2,128)(2,1)}, u32[]{:S(2)}, u32[]{:S(2)}) %all-to-all-start) | async-done | bytes 28704 | tf_op jit(solution)/shard_map/all_to_all | solution.py:168
  428.6 6.0 %all-to-all-start.5 = ((f32[64,1,1]{2,1,0:T(1,128)}), f32[64,1,1]{2,1,0:T(1,128)S(1)}, u32[]{:S(2)}, u32[]{:S(2)}) async-start(f32[64,1,1]{2,1,0:T(1,128)} %broadcast_in_dim.36), calls=%async_computation.5 | async-start | bytes 65536 | tf_op jit(solution)/shard_map/all_to_all | solution.py:57
  434.6 1.8 copy.128
  437.7 1.8 copy.131
  439.8 3.7 copy.114
  444.4 1.6 multiply_bitcast_fusion
  446.0 2.9 copy.129
  (71 shorter events, 24.4 us)
Async XLA Ops:
  7.2 135.9 %copy-start = (bf16[256,3584]{1,0:T(8,128)(2,1)S(1)}, bf16[256,3584]{1,0:T(8,128)(2,1)}, u32[]{:S(2)}) copy-start(bf16[256,3584]{1,0:T(8,128)(2,1)} %param.11) | copy-start | bytes 5505028
  7.2 135.2 %all-gather.5.cloned.1.call-start = ((), (), s32[]{:S(2)}) async-start(), calls=%async_computation.7 | async-start | bytes 3612672 | tf_op jit(solution)/shard_map/all_gather | solution.py:33
  24.3 185.5 %all-to-all-start.1 = ((bf16[64,896,56]{1,2,0:T(8,128)(2,1)}), bf16[64,896,56]{1,2,0:T(8,128)(2,1)}, u32[]{:S(2)}, u32[]{:S(2)}) async-start(bf16[64,896,56]{1,2,0:T(8,128)(2,1)} %stack.2), calls=%async_computation.1 | async-start | bytes 12845056 | tf_op jit(solution)/shard_map/all_to_all | solution.py:21
  37.8 105.3 %copy-start.4 = (bf16[3584,128]{1,0:T(8,128)(2,1)S(1)}, bf16[3584,128]{1,0:T(8,128)(2,1)}, u32[]{:S(2)}) copy-start(bf16[3584,128]{1,0:T(8,128)(2,1)} %param.14) | copy-start | bytes 2752516
  37.8 131.0 %all-gather.7.cloned.1.call-start = ((), (), s32[]{:S(2)}) async-start(), calls=%async_computation.8 | async-start | bytes 9633792 | tf_op jit(solution)/shard_map/all_gather | solution.py:33
  172.2 2.2 copy-start.9
  172.2 2.2 copy-start.11
  181.5 1.4 copy-start.6
  181.5 1.4 copy-start.7
  183.6 1.2 copy-start.2
  183.6 1.8 copy-start.13
  185.5 2.6 copy-start.12
  209.8 5.0 %copy-start.8 = (bf16[1,4,3584]{2,1,0:T(4,128)(2,1)S(1)}, bf16[1,4,3584]{2,1,0:T(4,128)(2,1)}, u32[]{:S(2)}) copy-start(bf16[1,4,3584]{2,1,0:T(4,128)(2,1)} %param.20) | copy-start | bytes 86020
  222.7 27.0 %all-to-all-start.2 = ((bf16[4,1,256,896]{3,2,1,0:T(8,128)(2,1)}), bf16[4,1,256,896]{3,2,1,0:T(8,128)(2,1)S(1)}, u32[]{:S(2)}, u32[]{:S(2)}) async-start(bf16[4,1,256,896]{3,2,1,0:T(8,128)(2,1)} %bitcast.101), calls=%async_computation.2 | async-start | bytes 3670016 | tf_op jit(solution)/shard_map/all_to_all | solution.py:51
  226.7 23.2 %copy-start.5 = (bf16[256,896]{1,0:T(8,128)(2,1)S(1)}, bf16[256,896]{1,0:T(8,128)(2,1)}, u32[]{:S(2)}) copy-start(bf16[256,896]{1,0:T(8,128)(2,1)} %param.12) | copy-start | bytes 1376260
  259.8 64.1 %all-to-all-start.4 = ((f32[64,1,1]{2,1,0:T(1,128)}), f32[64,1,1]{2,1,0:T(1,128)S(1)}, u32[]{:S(2)}, u32[]{:S(2)}) async-start(f32[64,1,1]{2,1,0:T(1,128)} %broadcast_in_dim.35), calls=%async_computation.4 | async-start | bytes 65536 | tf_op jit(solution)/shard_map/all_to_all | solution.py:57
  323.8 52.6 %all-to-all-start.6 = ((bf16[1,4,3584]{1,0,2:T(2,128)(2,1)}), bf16[1,4,3584]{1,0,2:T(2,128)(2,1)S(1)}, u32[]{:S(2)}, u32[]{:S(2)}) async-start(bf16[1,4,3584]{1,0,2:T(2,128)(2,1)} %copy.130), calls=%async_computation.6 | async-start | bytes 3670016 | tf_op jit(solution)/shard_map/all_to_all | solution.py:169
  331.1 2.0 copy-start.10
  376.5 51.5 %all-to-all-start = ((bf16[1,3584,4]{2,0,1:T(2,128)(2,1)}), bf16[1,3584,4]{2,0,1:T(2,128)(2,1)}, u32[]{:S(2)}, u32[]{:S(2)}) async-start(bf16[1,3584,4]{2,0,1:T(2,128)(2,1)} %copy.113), calls=%async_computation | async-start | bytes 3670016 | tf_op jit(solution)/shard_map/all_to_all | solution.py:168
  428.6 15.3 %all-to-all-start.5 = ((f32[64,1,1]{2,1,0:T(1,128)}), f32[64,1,1]{2,1,0:T(1,128)S(1)}, u32[]{:S(2)}, u32[]{:S(2)}) async-start(f32[64,1,1]{2,1,0:T(1,128)} %broadcast_in_dim.36), calls=%async_computation.5 | async-start | bytes 65536 | tf_op jit(solution)/shard_map/all_to_all | solution.py:57
  439.5 4.9 %copy-start.3 = (f32[64,3584]{0,1:T(8,128)S(1)}, f32[64,3584]{0,1:T(8,128)}, u32[]{:S(2)}) copy-start(f32[64,3584]{0,1:T(8,128)} %copy.128) | copy-start | bytes 2752516
  446.0 6.7 %copy-start.1 = (bf16[256,3584]{1,0:T(8,128)(2,1)S(1)}, bf16[256,3584]{1,0:T(8,128)(2,1)}, u32[]{:S(2)}) copy-start(bf16[256,3584]{1,0:T(8,128)(2,1)} %param.11) | copy-start | bytes 5505028
Sparse Core Ops, SparseCore 0:
  20.4 121.9 all-gather.4
  144.1 24.6 all-gather.6
